TPU v7x, 8 devices: a whole 2x2x1 slice. The times are simulated.
8 devices in a mesh: model: 2 (over z, y), data: 4 (over x, core).
Axes of the slice: x: 2, y: 2, z: 1, core: 2. Of those that a mesh axis runs over, the one named last changes fastest.
Arguments:
- h_a: bfloat16 [16384, 2048], P('data')
- h_b: bfloat16 [16384, 2048], P('data')
- w_one: bfloat16 [2048, 2048], P(None, 'model')
- w_two: bfloat16 [2048, 2048], P('model')
- w_three: bfloat16 [2048, 2048], P(None, 'model')
- g_one: float32 [2048], P('model')
- b_one: float32 [2048], P('model')
- g_two: float32 [2048], replicated
- b_two: float32 [2048], replicated
- lam_off: float32 [1], replicated
Outputs:
- output 1: float32 [1], replicated
- output 2: float32 [2048, 2048], P(None, 'model')
- output 3: float32 [2048, 2048], P('model')
- output 4: float32 [2048, 2048], P(None, 'model')
- output 5: float32 [2048], P('model')
- output 6: float32 [2048], P('model')
- output 7: float32 [2048], replicated
- output 8: float32 [2048], replicated
All inputs are finite; a program needn't handle non-finite values.
Results may differ from a plain program's by a relative error of at most 0.001.
Values are sent between devices in bfloat16 or wider.
A program may use at most 1 GiB of HBM per device.

v0:
```python
import jax
import jax.numpy as jnp
from jax import lax
from jax.sharding import PartitionSpec as P

BN_EPS = 1e-5


def batch_norm(pre_act, total_rows):
    local_sums = jnp.stack([jnp.sum(pre_act, axis=1, keepdims=True), jnp.sum(pre_act * pre_act, axis=1, keepdims=True)])
    moments = lax.psum(local_sums, 'data') / total_rows
    inv_std = lax.rsqrt(moments[1] - moments[0] * moments[0] + BN_EPS)
    return (pre_act - moments[0]) * inv_std, inv_std


def bn_backward(d_act, lin_val, norm_val, inv_std, gamma_vec, total_rows):
    d_lin = jnp.where(lin_val > 0, d_act, 0.0)
    local_sums = jnp.stack([jnp.sum(d_lin, axis=1, keepdims=True), jnp.sum(d_lin * norm_val, axis=1, keepdims=True)])
    global_sums = lax.psum(local_sums, 'data')
    d_pre = gamma_vec * inv_std * (d_lin - (global_sums[0] + norm_val * global_sums[1]) / total_rows)
    return d_pre.astype(jnp.bfloat16), jnp.sum(global_sums[1], axis=(0, 1)), jnp.sum(global_sums[0], axis=(0, 1))


def solution(mesh):
    data_size = mesh.shape['data']

    def shard_body(h_a, h_b, w_one, w_two, w_three, g_one, b_one, g_two, b_two, lam_off):
        local_rows = h_a.shape[0]
        total_rows = local_rows * data_size
        full_dim, feat_dev = w_three.shape
        view_feats = jnp.stack([h_a, h_b])
        pre_one = jnp.einsum('vnf,fd->vnd', view_feats, w_one, preferred_element_type=jnp.float32)
        norm_one, inv_one = batch_norm(pre_one, total_rows)
        lin_one = g_one * norm_one + b_one
        act_one = jnp.maximum(lin_one, 0.0).astype(jnp.bfloat16)
        pre_two = lax.psum(jnp.einsum('woe,ef->wof', act_one, w_two, preferred_element_type=jnp.float32), 'model')
        norm_two, inv_two = batch_norm(pre_two, total_rows)
        lin_two = g_two * norm_two + b_two
        act_two = jnp.maximum(lin_two, 0.0).astype(jnp.bfloat16)
        pre_out = jnp.einsum('woe,ef->wof', act_two, w_three, preferred_element_type=jnp.float32)
        norm_out, inv_out = batch_norm(pre_out, total_rows)
        embed_bf = norm_out.astype(jnp.bfloat16)
        emb_b_full = lax.all_gather(embed_bf[1], 'model', axis=1, tiled=True)
        corr_part = jnp.einsum('ni,nj->ij', embed_bf[0], emb_b_full, preferred_element_type=jnp.float32)
        corr_mat = lax.psum(corr_part, 'data') / total_rows
        row_ids = lax.axis_index('model') * feat_dev + lax.broadcasted_iota(jnp.int32, (feat_dev, 1), 0)
        col_ids = lax.broadcasted_iota(jnp.int32, (1, full_dim), 1)
        is_diag = row_ids == col_ids
        lam_val = lam_off[0]
        loss_part = jnp.sum(jnp.where(is_diag, (1.0 - corr_mat) * (1.0 - corr_mat), lam_val * corr_mat * corr_mat))
        loss_val = lax.psum(loss_part, 'model')
        grad_c = jnp.where(is_diag, -2.0 * (1.0 - corr_mat), 2.0 * lam_val * corr_mat).astype(jnp.bfloat16)
        d_emb_a = jnp.einsum('nj,ij->ni', emb_b_full, grad_c, preferred_element_type=jnp.float32)
        d_part_b = jnp.einsum('ni,ij->nj', embed_bf[0], grad_c, preferred_element_type=jnp.float32)
        d_emb_b = lax.psum_scatter(d_part_b, 'model', scatter_dimension=1, tiled=True)
        d_emb = jnp.stack([d_emb_a, d_emb_b]) / total_rows
        embed_f = embed_bf.astype(jnp.float32)
        grad_sums = jnp.stack([jnp.sum(d_emb, axis=1, keepdims=True), jnp.sum(d_emb * embed_f, axis=1, keepdims=True)])
        grad_moments = lax.psum(grad_sums, 'data') / total_rows
        d_out = (inv_out * (d_emb - grad_moments[0] - embed_f * grad_moments[1])).astype(jnp.bfloat16)
        dw_three = lax.psum(jnp.einsum('woe,wof->ef', act_two, d_out, preferred_element_type=jnp.float32), 'data')
        d_act_two = lax.psum(jnp.einsum('wof,ef->woe', d_out, w_three, preferred_element_type=jnp.float32), 'model')
        d_pre_two, dg_two, db_two = bn_backward(d_act_two, lin_two, norm_two, inv_two, g_two, total_rows)
        dw_two = lax.psum(jnp.einsum('woe,wof->ef', act_one, d_pre_two, preferred_element_type=jnp.float32), 'data')
        d_act_one = jnp.einsum('wof,ef->woe', d_pre_two, w_two, preferred_element_type=jnp.float32)
        d_pre_one, dg_one, db_one = bn_backward(d_act_one, lin_one, norm_one, inv_one, g_one, total_rows)
        dw_one = lax.psum(jnp.einsum('vnf,vnd->fd', view_feats, d_pre_one, preferred_element_type=jnp.float32), 'data')
        return loss_val.reshape(1), dw_one, dw_two, dw_three, dg_one, db_one, dg_two, db_two

    in_specs = (P('data', None), P('data', None), P(None, 'model'), P('model', None), P(None, 'model'),
                P('model'), P('model'), P(), P(), P())
    out_specs = (P(), P(None, 'model'), P('model', None), P(None, 'model'), P('model'), P('model'), P(), P())
    return jax.shard_map(shard_body, mesh=mesh, in_specs=in_specs, out_specs=out_specs, check_vma=False)
```

profile of v0, /device:TPU:0, one launch (start us, length us, event | category | flops | bytes accessed | tf_op | source)
XLA Modules:
  0.0 4705.8 jit_solution(10838742300922571541)
XLA Ops:
  7.2 44.2 fusion.48
  51.5 13.7 psum.91
  65.8 46.6 fusion.28
  112.5 1451.6 %all-reduce.6.cloned.1.call-done = f32[2,4096,2048]{2,1,0:T(8,128)} async-done(((f32[2,4096,2048]{2,1,0:T(8,128)}), f32[2,4096,2048]{2,1,0:T(8,128)}) %all-reduce.6.cloned.1.call-update) | async-done | bytes 67108880 | tf_op jit(solution)/shard_map/psum | solution.py:36
  1564.1 21.2 fusion.45
  1597.3 47.0 fusion.47
  1654.5 18.1 multiply_convert_fusion.2
  1680.7 198.0 %all-gather.3.cloned.1.call-done = bf16[1,4096,2048]{2,1,0:T(8,128)(2,1)} async-done(((bf16[1,4096,1024]{2,1,0:T(8,128)(2,1)}), bf16[1,4096,2048]{2,1,0:T(8,128)(2,1)}) %all-gather.3.cloned.1.call-update) | async-done | bytes 16777232 | tf_op jit(solution)/shard_map/all_gather | solution.py:43
  1878.7 24.1 fusion.10
  1903.5 146.5 %all-reduce.8.cloned.1.call-done = f32[1024,2048]{1,0:T(8,128)} async-done(((f32[1024,2048]{1,0:T(8,128)}), f32[1024,2048]{1,0:T(8,128)}) %all-reduce.8.cloned.1.call-update) | async-done | bytes 8388624 | tf_op jit(solution)/shard_map/psum | solution.py:45
  2050.1 27.2 fusion.21
  2077.6 25.8 fusion.18
  2103.5 340.3 %reduce-scatter.2.cloned.1.call-done = f32[4096,1024]{1,0:T(8,128)} async-done(((f32[4096,2048]{1,0:T(8,128)}), f32[4096,1024]{1,0:T(8,128)}) %reduce-scatter.2.cloned.1.call-update) | async-done | bytes 16777232 | tf_op jit(solution)/shard_map/reduce_scatter | solution.py:55
  2443.7 21.6 fusion.7
  2476.0 28.5 fusion.3
  2504.5 43.3 fusion.23
  2548.6 46.3 convolution_bitcast_fusion
  2594.9 1404.2 %all-reduce.10.cloned.1.call-done = f32[2,4096,2048]{2,1,0:T(8,128)} async-done(((f32[2,4096,2048]{2,1,0:T(8,128)}), f32[2,4096,2048]{2,1,0:T(8,128)}) %all-reduce.10.cloned.1.call-update) | async-done | bytes 67108880 | tf_op jit(solution)/shard_map/psum | solution.py:62
  3999.1 41.5 fusion.6
  4052.6 53.6 %multiply_convert_fusion = bf16[2,4096,2048]{2,1,0:T(8,128)(2,1)} fusion(f32[2,4096,2048]{2,1,0:T(8,128)} %all-reduce.6.cloned.1.call-done, f32[2,2048]{1,0:T(2,128)S(1)} %get-tuple-element.27, f32[2,2048]{1,0:T(2,128)S(1)} %get-tuple-element.28, f32[2,2048]{1,0:T(2,128)S(1)} %copy-done.6, f32[2,2048]{1,0:T(2,128)S(1)} %copy-done.3, ...), kind=kLoop, calls=%fused_computation | loop fusion | flops 201326592 | bytes 167870464 | tf_op jit(solution)/shard_map/convert_element_type | solution.py:21
  4106.2 44.3 convolution_bitcast_fusion.1
  4150.5 51.4 %fusion.46 = (f32[2,1024]{1,0:T(2,128)S(1)}, f32[2,1024]{1,0:T(2,128)S(1)}, f32[2,4096,1024]{2,1,0:T(8,128)}) fusion(f32[2,1024]{1,0:T(2,128)S(1)} %copy-done.15, f32[2,4096,1024]{2,1,0:T(8,128)} %get-tuple-element.37, f32[2,1024]{1,0:T(2,128)S(1)} %copy-done.12, bf16[2,4096,2048]{2,1,0:T(8,128)(2,1)} %multiply_convert_fusion, ...), kind=kOutput, calls=%fused_computation.97 | convolution fusion | flops 34435235840 | bytes 104898560 | tf_op jit(solution)/shard_map/wof,ef->woe/dot_general | solution.py:65
  4213.0 47.1 %fusion.22 = f32[2048,1024]{1,0:T(8,128)} fusion(f32[2,4096,1024]{2,1,0:T(8,128)} %get-tuple-element.39, f32[2,4096,1024]{2,1,0:T(8,128)} %get-tuple-element.37, f32[2,1024]{1,0:T(2,128)S(1)} %get-tuple-element.31, f32[2,1024]{1,0:T(2,128)S(1)} %get-tuple-element.32, f32[2,1024]{1,0:T(2,128)S(1)} %copy-done.13, f32[2,1024]{1,0:T(2,128)S(1)} %copy-done.15, ...), kind=kOutput, calls=%fused_computation.44 | convolution fusion | flops 34443624448 | bytes 109092864 | tf_op jit(solution)/shard_map/vnf,vnd->fd/dot_general | solution.py:67
  4271.9 406.9 %all-reduce.12.cloned.1.call-done = (f32[2048,1024]{1,0:T(8,128)}, f32[1024,2048]{1,0:T(8,128)}, f32[2048,1024]{1,0:T(8,128)}) async-done(((f32[2048,1024]{1,0:T(8,128)}, f32[1024,2048]{1,0:T(8,128)}, f32[2048,1024]{1,0:T(8,128)}), (f32[2048,1024]{1,0:T(8,128)}, f32[1024,2048]{1,0:T(8,128)}, f32[2048,1024]{1,0:T(8,128)})) %all-reduce.12.cloned.1.call-update) | async-done | bytes 25165840 | tf_op jit(solution)/shard_map/psum | solution.py:67
  (88 shorter events, 97.4 us)
Async XLA Ops:
  7.2 1556.9 %all-reduce.6.cloned.1.call-start = ((), (), s32[]{:S(2)}) async-start(), calls=%async_computation.1 | async-start | bytes 134217728 | tf_op jit(solution)/shard_map/psum | solution.py:36
  7.2 57.9 %copy-start.16 = (f32[1024]{0:T(1024)S(1)}, f32[1024]{0:T(1024)}, u32[]{:S(2)}) copy-start(f32[1024]{0:T(1024)} %param.15) | copy-start | bytes 12292
  7.2 58.5 %copy-start.18 = (f32[1024]{0:T(1024)S(1)}, f32[1024]{0:T(1024)}, u32[]{:S(2)}) copy-start(f32[1024]{0:T(1024)} %param.16) | copy-start | bytes 12292
  65.1 47.2 %copy-start.11 = (f32[2,1024]{1,0:T(2,128)}, f32[2,1024]{1,0:T(2,128)S(1)}, u32[]{:S(2)}) copy-start(f32[2,1024]{1,0:T(2,128)S(1)} %slice_bitcast_fusion.12) | copy-start | bytes 24580
  65.8 46.6 copy-start.14
  112.4 1484.3 %copy-start.4 = (f32[2048]{0:T(1024)S(1)}, f32[2048]{0:T(1024)}, u32[]{:S(2)}) copy-start(f32[2048]{0:T(1024)} %param.17) | copy-start | bytes 24580
  112.4 1484.9 %copy-start.7 = (f32[2048]{0:T(1024)S(1)}, f32[2048]{0:T(1024)}, u32[]{:S(2)}) copy-start(f32[2048]{0:T(1024)} %param.18) | copy-start | bytes 24580
  112.4 1766.3 %all-gather.3.cloned.1.call-start = ((), (), s32[]{:S(2)}) async-start(), calls=%async_computation.5 | async-start | bytes 25165824 | tf_op jit(solution)/shard_map/all_gather | solution.py:43
  1596.7 47.6 %copy-start = (f32[2,2048]{1,0:T(2,128)}, f32[2,2048]{1,0:T(2,128)S(1)}, u32[]{:S(2)}) copy-start(f32[2,2048]{1,0:T(2,128)S(1)} %slice_bitcast_fusion.4) | copy-start | bytes 49156
  1597.3 47.0 copy-start.2
  1680.5 369.6 %all-reduce.8.cloned.1.call-start = ((), (), s32[]{:S(2)}) async-start(), calls=%async_computation.2 | async-start | bytes 16777216 | tf_op jit(solution)/shard_map/psum | solution.py:45
  1902.8 540.9 %reduce-scatter.2.cloned.1.call-start = ((), (), s32[]{:S(2)}) async-start(), calls=%async_computation.3 | async-start | bytes 50331648 | tf_op jit(solution)/shard_map/reduce_scatter | solution.py:55
  1903.5 174.1 %copy-start.9 = (s32[1024]{0:T(1024)}, s32[1024]{0:T(1024)S(1)}, u32[]{:S(2)}) copy-start(s32[1024]{0:T(1024)S(1)} %iota_add_fusion) | copy-start | bytes 12292
  2077.3 1921.8 %all-reduce.10.cloned.1.call-start = ((), (), s32[]{:S(2)}) async-start(), calls=%async_computation.4 | async-start | bytes 134217728 | tf_op jit(solution)/shard_map/psum | solution.py:62
  2547.9 2130.9 %all-reduce.12.cloned.1.call-start = ((), (), s32[]{:S(2)}) async-start(), calls=%async_computation.6 | async-start | bytes 50331648 | tf_op jit(solution)/shard_map/psum | solution.py:67
  2594.9 1457.6 %copy-start.6 = (f32[2,2048]{1,0:T(2,128)S(1)}, f32[2,2048]{1,0:T(2,128)}, u32[]{:S(2)}) copy-start(f32[2,2048]{1,0:T(2,128)} %get-tuple-element.29) | copy-start | bytes 49156
  4052.5 53.6 %copy-start.12 = (f32[2,1024]{1,0:T(2,128)S(1)}, f32[2,1024]{1,0:T(2,128)}, u32[]{:S(2)}) copy-start(f32[2,1024]{1,0:T(2,128)} %copy-done.11) | copy-start | bytes 24580
  4052.5 53.6 %copy-start.15 = (f32[2,1024]{1,0:T(2,128)S(1)}, f32[2,1024]{1,0:T(2,128)}, u32[]{:S(2)}) copy-start(f32[2,1024]{1,0:T(2,128)} %copy-done.14) | copy-start | bytes 24580
  4052.6 53.6 %copy-start.17 = (f32[1024]{0:T(1024)S(1)}, f32[1024]{0:T(1024)}, u32[]{:S(2)}) copy-start(f32[1024]{0:T(1024)} %param.15) | copy-start | bytes 12292
  4052.6 53.6 %copy-start.19 = (f32[1024]{0:T(1024)S(1)}, f32[1024]{0:T(1024)}, u32[]{:S(2)}) copy-start(f32[1024]{0:T(1024)} %param.16) | copy-start | bytes 12292
  4150.5 62.5 %copy-start.13 = (f32[2,1024]{1,0:T(2,128)S(1)}, f32[2,1024]{1,0:T(2,128)}, u32[]{:S(2)}) copy-start(f32[2,1024]{1,0:T(2,128)} %get-tuple-element.33) | copy-start | bytes 24580
  4213.0 47.2 %copy-start.10 = (s32[1024]{0:T(1024)S(1)}, s32[1024]{0:T(1024)}, u32[]{:S(2)}) copy-start(s32[1024]{0:T(1024)} %copy-done.9) | copy-start | bytes 12292
  4678.8 16.5 slice-start
  4678.8 16.5 slice-start.1
  (4 other events, 2.9 us)
Sparse Core Ops, SparseCore 0:
  112.5 1451.4 all-reduce.5
  1680.6 198.0 all-gather.2
  1902.9 147.1 all-reduce.7
  2077.4 366.2 reduce-scatter.1
  2548.0 1451.0 all-reduce.9
  4260.3 418.4 all-reduce.11
where the time goes:
time: 4710 us
  waiting for transfers between devices  3950 us (84%)
  matrix products  447 us (9%)
  other arithmetic  193 us (4%)
  blocking collectives  73.6 us (2%)
    psum x1, waiting for transfers between devices, shard_body(): lax.psum(jnp.einsum('woe,ef->wof', act_one, w_two, preferred_element_type...  1450 us
    psum x1, waiting for transfers between devices, shard_body(): lax.psum(jnp.einsum('wof,ef->woe', d_out, w_three, preferred_element_type...  1400 us
    psum x1, waiting for transfers between devices, shard_body(): lax.psum(jnp.einsum('vnf,vnd->fd', view_feats, d_pre_one, preferred_eleme...  407 us
    reduce_scatter x1, waiting for transfers between devices, shard_body(): lax.psum_scatter(d_part_b, 'model', scatter_dimension=1, tiled=True)  340 us
    all_gather x1, waiting for transfers between devices, shard_body(): emb_b_full = lax.all_gather(embed_bf[1], 'model', axis=1, tiled=True)  198 us
    psum x1, waiting for transfers between devices, shard_body(): corr_mat = lax.psum(corr_part, 'data') / total_rows  147 us
  transfers between devices with their start and end apart: 6, of which 6 were waited for; matrix products, arithmetic and copies ran while one was open for 2% of the time, Pallas kernels for 0%

commit v1 on v0

v1 whole, which is shorter than its diff:
```python
import jax
import jax.numpy as jnp
from jax import lax
from jax.experimental import pallas as pl
from jax.experimental.pallas import tpu as pltpu
from jax.sharding import PartitionSpec as P

BN_EPS = 1e-5
F32 = jnp.float32
BF16 = jnp.bfloat16
TM = 512
MAX_VMEM = 67043328
ANY = pl.BlockSpec(memory_space=pl.ANY)
VMEM = pl.BlockSpec(memory_space=pltpu.VMEM)
DMA = pltpu.SemaphoreType.DMA
TWO_DMA = DMA((2,))
BOTH = (0, 1)
PEERS = [(ky, kx, kc) for ky in BOTH for kx in BOTH for kc in BOTH][1:]
C_PEER, X_PEER, Y_PEER = PEERS[0], PEERS[1], PEERS[3]
N_DEV = len(PEERS) + 1


def mm(left, right):
    return jnp.dot(left, right, preferred_element_type=F32)


def mm_bt(left, right):
    return lax.dot_general(left, right, (((1,), (1,)), ((), ())), preferred_element_type=F32)


def mm_at(left, right):
    return lax.dot_general(left, right, (((0,), (0,)), ((), ())), preferred_element_type=F32)


def other(p):
    return 1 - p


def odd(i):
    return lax.rem(i, 2)


def split(i):
    return lax.div(i, 2), odd(i)


def loop(n, body, start=0):
    def one(i, carry):
        body(i)
        return carry

    lax.fori_loop(start, n, one, 0)


def whole(*shape):
    return pl.BlockSpec(shape, lambda *_: (0,) * len(shape))


def at(i, n):
    return pl.ds(pl.multiple_of(i * n, n), n)


def sds(shape, dtype):
    return jax.ShapeDtypeStruct(shape, dtype)


def mean_inv(sums, total):
    mean = sums[:1] / total
    var = sums[1:2] / total - mean * mean
    return mean, lax.rsqrt(var + BN_EPS)


def two_sums(one, two):
    return jnp.concatenate([jnp.sum(one, axis=0, keepdims=True), jnp.sum(two, axis=0, keepdims=True)], axis=0)


def coords():
    y, d = lax.axis_index('model'), lax.axis_index('data')
    return y, lax.div(d, 2), odd(d)


def flip(here, which):
    return tuple(other(p) if f else p for p, f in zip(here, which))


def flat(here):
    y, x, c = here
    return 4 * y + 2 * x + c


def device(here):
    y, x, c = here
    return (y, 2 * x + c)


def remote(src, dst, send_sem, recv_sem, there):
    return pltpu.make_async_remote_copy(
        src_ref=src, dst_ref=dst, send_sem=send_sem, recv_sem=recv_sem, device_id=device(there),
        device_id_type=pl.DeviceIdType.MESH)


def arrive():
    here = coords()
    for k in PEERS:
        pl.semaphore_signal(pltpu.get_barrier_semaphore(), inc=1, device_id=device(flip(here, k)),
                            device_id_type=pl.DeviceIdType.MESH)


def all_arrived():
    pl.semaphore_wait(pltpu.get_barrier_semaphore(), len(PEERS))


class Share:
    def __init__(self, acc, got, send_sem, recv_sem):
        self.acc, self.got, self.send_sem, self.recv_sem = acc, got, send_sem, recv_sem

    @staticmethod
    def scratch(n, *shape):
        return [pltpu.VMEM((n, *shape), F32), pltpu.VMEM((n, N_DEV, *shape), F32), DMA((n,)), DMA((n,))]

    def start(self, b):
        here = coords()
        me = flat(here)
        self.got[b, me] = self.acc[b]
        for which in PEERS:
            remote(self.acc.at[b], self.got.at[b, me], self.send_sem.at[b], self.recv_sem.at[b],
                   flip(here, which)).start()

    def total(self, b):
        all_of = self.got.at[b, pl.ds(0, len(PEERS))]
        copies = remote(all_of, all_of, self.send_sem.at[b], self.recv_sem.at[b], coords())
        copies.wait_send()
        copies.wait_recv()
        out = self.got[b, 0]
        for f in range(1, N_DEV):
            out += self.got[b, f]
        return out


class Gather:
    def __init__(self, own, dest, n, sems):
        self.own, self.dest, self.n = own, dest, n
        self.ys, self.yr, self.xs, self.xr, self.cs, self.cr = sems
        self.here = coords()
        _, x, c = self.here
        self.mine, self.across = 2 * x + c, 2 * (other(x)) + c
        self.core = (2 * x + other(c), 2 * (other(x)) + other(c))

    @staticmethod
    def scratch(n):
        return [DMA((n,))] * 4 + [DMA((2, n))] * 2

    def y(self, p):
        model = self.here[0]
        return remote(self.own(self.mine, p), self.dest(model, self.mine, p), self.ys.at[p], self.yr.at[p],
                      flip(self.here, Y_PEER))

    def moved(self, q, p, send_sem, recv_sem, which):
        ref = self.dest(1 - self.here[0], q, p)
        return remote(ref, ref, send_sem, recv_sem, flip(self.here, which))

    def x(self, p, q):
        return self.moved(q, p, self.xs.at[p], self.xr.at[p], X_PEER)

    def c(self, p, late, q):
        return self.moved(q, p, self.cs.at[late, p], self.cr.at[late, p], C_PEER)

    def start(self):
        for p in range(self.n):
            self.y(p).start()

    def pass_y(self, p):
        self.moved(self.mine, p, self.ys.at[p], self.yr.at[p], Y_PEER).wait_recv()
        self.x(p, self.mine).start()
        self.c(p, 0, self.mine).start()

    def pass_x(self, p):
        self.x(p, self.across).wait_recv()
        self.c(p, 1, self.across).start()

    def wait_core(self, late):
        for p in range(self.n):
            self.c(p, late, self.core[late]).wait_recv()

    def drain(self):
        for p in range(self.n):
            self.y(p).wait_send()
            self.x(p, self.mine).wait_send()
            self.c(p, 0, self.mine).wait_send()
            self.c(p, 1, self.across).wait_send()


def call(kernel, name, cid, grid, in_specs, out_specs, out_shape, scratch, flops, nbytes, args):
    return pl.pallas_call(
        kernel, name=name, grid=grid, in_specs=in_specs, out_specs=out_specs, out_shape=out_shape, scratch_shapes=scratch,
        compiler_params=pltpu.CompilerParams(vmem_limit_bytes=MAX_VMEM, collective_id=cid, has_side_effects=cid is not None),
        cost_estimate=pl.CostEstimate(flops=flops, bytes_accessed=nbytes, transcendentals=0))(*args)


def fwd_first(h_a, h_b, w_one, w_two, gb_own):
    depth, half = w_one.shape
    dim = 2 * half
    rows = h_a.shape[0] // 2
    tile, width, quarter = 2 * TM, half // 2, half // 4
    steps = rows // tile
    per_block = 2 * steps
    n = 4

    def block(j):
        y, x, _ = coords()
        return jnp.where(j < 2, 2 * y + j, 2 * (other(y)) + jnp.where(j == 2, x, other(x)))

    def kernel(ha_ref, hb_ref, w_ref, w2_ref, gb_ref, u_ref, s_ref, gbo_ref, w2o_ref, w1, gbf, *sems):
        share, sems = Share(*sems[:4]), sems[4:]
        gs, gr, lsem = sems[:3]
        sems = sems[3:]
        j, i = pl.program_id(0), pl.program_id(1)
        step = j * per_block + i
        here = coords()
        y = here[0]
        one = Gather(lambda q, p: w_ref.at[at(p, depth // n), at(q, quarter)],
                     lambda m, q, p: w1.at[at(p, depth // n), at(m * 4 + q, quarter)], n, sems[:6])
        two = Gather(lambda q, p: w2_ref.at[at(q * n + p, quarter // n)],
                     lambda m, q, p: w2o_ref.at[at(q * n + p, quarter // n)], n, sems[6:])

        def local(b):
            return pltpu.make_async_copy(w_ref.at[:, at(b, width)], w1.at[:, at(2 * y + b, width)], lsem.at[b])

        def bn_vectors(m):
            return remote(gb_ref, gbf.at[:, at(m, half)], gs, gr, flip(here, Y_PEER))

        def begin():
            arrive()
            local(0).start()
            local(1).start()
            all_arrived()
            one.start()
            two.start()
            bn_vectors(y).start()
            local(0).wait()

        def late_half():
            for p in range(2, n):
                one.pass_y(p)
            one.pass_x(0)
            one.pass_x(1)
            one.wait_core(0)

        def between():
            one.pass_x(2)
            two.pass_y(0)

        def last_block():
            one.pass_x(n - 1)
            one.wait_core(1)
            two.pass_y(1)
            two.pass_x(0)

        hooks = {0: begin, 3: lambda: one.pass_y(0), per_block: lambda: local(1).wait(), 6: lambda: one.pass_y(1),
                 2 * per_block: late_half, 10: between, 3 * per_block: last_block,
                 14: lambda: two.pass_y(2), 15: lambda: two.pass_x(1)}
        for s in sorted(hooks):
            pl.when(step == s)(hooks[s])
        for b in range(3):
            pl.when(step == (b + 1) * per_block)(lambda b=b: share.start(block(b)))

        h = lax.select(i < steps, ha_ref[...], hb_ref[...])
        u = mm(h, w1[:, at(block(j), width)])
        u_ref[...] = u
        sums = two_sums(u, u * u)
        v = i // steps
        share.acc[block(j), v] = jnp.where(i % steps == 0, 0.0, share.acc[block(j), v]) + sums

        @pl.when(step == 4 * per_block - 1)
        def _():
            share.start(block(3))
            two.pass_y(n - 1)
            for p in range(2, n):
                two.pass_x(p)
            bn_vectors(other(y)).wait_recv()
            bn_vectors(y).wait_send()
            gbo_ref[...] = gbf[...]
            gbo_ref[:, at(y, half)] = gb_ref[...]
            for b in range(4):
                s_ref[:, :, b * width:(b + 1) * width] = share.total(b)
            one.drain()
            two.drain()
            two.wait_core(0)
            two.wait_core(1)

    return call(
        kernel, "fwd_first", 0, (4, per_block),
        [pl.BlockSpec((tile, depth), lambda j, i: (coords()[0] * steps + jnp.minimum(i, steps - 1), 0)),
         pl.BlockSpec((tile, depth), lambda j, i: (coords()[0] * steps + jnp.maximum(i - steps, 0), 0)),
         ANY, ANY, whole(2, half)],
        [pl.BlockSpec((tile, width), lambda j, i: (i, block(j))), whole(2, 2, dim),
         whole(2, dim), ANY],
        [sds((2 * rows, dim), F32), sds((2, 2, dim), F32), sds((2, dim), F32), sds((half, dim), BF16)],
        [pltpu.VMEM((depth, dim), BF16), pltpu.VMEM((2, dim), F32)] + Share.scratch(4, 2, 2, width)
        + [DMA, DMA, TWO_DMA] + Gather.scratch(n) * 2,
        4 * rows * depth * dim, 2 * rows * (8 * depth + 4 * dim), (h_a, h_b, w_one, w_two, gb_own))


def fwd_next(u, sums, gb, w_own, w_other, by_rows, total, cid, w_next=None):
    all_rows, depth = u.shape
    dim = w_own.shape[1] if by_rows else 2 * w_own.shape[1]
    half = dim // 2
    quarter = half // 4
    steps = all_rows // 2 // TM
    last = 2 * steps - 1
    slab = dim // (2 * steps)
    n = 4

    def kernel(u_ref, s_ref, gb_ref, wo_ref, wt_ref, *refs):
        if w_next is not None:
            wn_ref, refs = refs[0], refs[1:]
        x_ref, o_ref, so_ref, wtr_ref, *refs = refs
        if w_next is not None:
            wno_ref, *refs = refs
        w, acc, got, ssem, rsem, lsem, *refs = refs
        share = Share(acc, got, ssem, rsem)
        i = pl.program_id(0)
        y = coords()[0]

        def local(ref, model, b):
            where = at(model, half)
            return pltpu.make_async_copy(ref, w.at[where] if by_rows else w.at[:, where], lsem.at[b])

        if w_next is not None:
            gather = Gather(lambda q, p: wn_ref.at[at(p, depth // n), at(q, quarter)],
                            lambda m, q, p: wno_ref.at[at(p, depth // n), at(q, quarter)], n, refs)

        @pl.when(i == 0)
        def _():
            arrive()
            local(wo_ref, y, 0).start()
            local(wt_ref, other(y), 1).start()
            all_arrived()
            if w_next is not None:
                gather.start()
            local(wo_ref, y, 0).wait()
            local(wt_ref, other(y), 1).wait()

        if w_next is not None:
            for p in range(n):
                pl.when(i == p + 1)(lambda p=p: gather.pass_y(p))
                pl.when(i == p + 3)(lambda p=p: gather.pass_x(p))
        pl.when(i == steps)(lambda: share.start(0))

        mean, inv = mean_inv(s_ref[0], total)
        act = jnp.maximum((u_ref[...] - mean) * inv * gb_ref[:1] + gb_ref[1:], 0.0).astype(BF16)
        x_ref[...] = act
        out = mm(act, w[...])
        o_ref[...] = out
        wtr_ref[...] = w[:, at(i, slab)].T
        v = i // steps
        share.acc[v] = jnp.where(i % steps == 0, 0.0, share.acc[v]) + two_sums(out, out * out)

        @pl.when(i == last)
        def _():
            share.start(1)
            for b in BOTH:
                so_ref[b] = share.total(b)
            if w_next is not None:
                gather.drain()
                gather.wait_core(0)
                gather.wait_core(1)

    more = w_next is not None
    return call(
        kernel, "fwd_next", cid, (2 * steps,),
        [pl.BlockSpec((TM, depth), lambda i: (i, 0)), pl.BlockSpec((1, 2, depth), lambda i: (i // steps, 0, 0)),
         whole(2, depth), ANY, ANY] + [ANY] * more,
        [pl.BlockSpec((TM, depth), lambda i: (i, 0)), pl.BlockSpec((TM, dim), lambda i: (i, 0)),
         whole(2, 2, dim), pl.BlockSpec((slab, depth), lambda i: (i, 0))] + [ANY] * more,
        [sds((all_rows, depth), BF16), sds((all_rows, dim), F32), sds((2, 2, dim), F32), sds((dim, depth), BF16)]
        + ([sds(w_next.shape, BF16)] if more else []),
        [pltpu.VMEM((depth, dim), BF16)] + Share.scratch(2, 2, dim) + [TWO_DMA] + (Gather.scratch(n) if more else []),
        2 * all_rows * depth * dim, all_rows * (6 * depth + 4 * dim),
        (u, sums, gb, w_own, w_other) + ((w_next,) if more else ()))


def corr_grad(z, sums, lam, total):
    all_rows, dim = z.shape
    rows = all_rows // 2
    half = dim // 2
    quart = half // 2
    n_chunk = 8
    width = half // n_chunk
    pair = 2 * width
    zt = mt = TM
    z_steps = all_rows // zt
    m_steps = rows // mt
    scale = 1.0 / total

    def kernel(z_ref, s_ref, lam_ref, zho_ref, d_ref, so_ref, zh, da, ck, r1, r2, g, stage, acc, got, ssem, rsem, zs, zos,
               d1s, d1r, s1s, s1r, s2s, s2r, a2s, a2r, a1s, a1r, ads, adr, dbs, das):
        share = Share(acc, got, ssem, rsem)
        here = coords()
        y, x, c = here
        on_x = c == 0
        by_core = lambda one, two: tuple(jnp.where(on_x, a, b) for a, b in zip(one, two))
        first = by_core(flip(here, X_PEER), flip(here, Y_PEER))
        second = by_core(flip(here, Y_PEER), flip(here, X_PEER))
        cpeer = flip(here, C_PEER)
        bit1, bit2 = by_core((x, y), (y, x))
        arrive()
        acc[...] = jnp.zeros_like(acc)

        def load(i, slot):
            return pltpu.make_async_copy(z_ref.at[at(i, zt)], ck.at[at(slot, zt)], zs.at[slot])

        def zh_out(v, r, i):
            return pltpu.make_async_copy(zh.at[v, at(r, zt)], zho_ref.at[v, at(r, zt)], zos.at[i])

        load(0, 0).start()

        def normalise(i):
            slot = odd(i)
            v, r = lax.div(i, z_steps // 2), lax.rem(i, z_steps // 2)
            pl.when(i + 1 < z_steps)(lambda: load(i + 1, other(slot)).start())
            load(i, slot).wait()
            mean, inv = mean_inv(s_ref[v], total)
            zh[v, at(r, zt)] = ((ck[at(slot, zt)] - mean) * inv).astype(BF16)
            zh_out(v, r, i).start()

        loop(z_steps, normalise)
        all_arrived()

        def both(v, rows_at, t):
            return jnp.concatenate([zh[v, rows_at, at(b * n_chunk + t, width)] for b in BOTH], axis=1)

        every, upper, lower = pl.ds(0, rows), pl.ds(0, half), pl.ds(half, half)
        group = lambda t, b: at(2 * t + b, width)

        def to_core(t):
            return remote(da.at[lower, at(t, pair)], da.at[upper, at(t, pair)], d1s.at[t], d1r.at[t], cpeer)

        def to_first(t):
            return remote(ck.at[:, group(t, other(bit1))], r1.at[t], s1s.at[t], s1r.at[t], first)

        def to_second(t):
            return remote(ck.at[at(other(bit2), quart), group(t, bit1)], r2.at[t], s2s.at[t], s2r.at[t], second)

        def g_second(t, b):
            block = g.at[t, at(2 * c + b, quart), at(bit1, width)]
            return remote(block, block, a2s.at[t], a2r.at[t], second)

        def g_first(t, b):
            block = g.at[t, at(c, half), at(b, width)]
            return remote(block, block, a1s.at[t], a1r.at[t], first)

        def g_core(t, core):
            block = g.at[t, at(core, half)]
            return remote(block, block, ads.at[t], adr.at[t], cpeer)

        def chip_sum(t):
            to_core(t).wait_recv()
            ck[:, at(t, pair)] += da[upper, at(t, pair)]

        def corr_part(t):
            right = both(1, every, t)
            da[lower, at(t, pair)] = mm_at(zh[0, :, at(other(c), half)], right)
            ck[:, at(t, pair)] = mm_at(zh[0, :, at(c, half)], right)
            to_core(t).start()

            @pl.when(t > 0)
            def _():
                chip_sum(t - 1)
                pl.when(t <= 2)(lambda: to_first(t - 1).start())


        loop(n_chunk, corr_part)
        chip_sum(n_chunk - 1)
        for t in range(n_chunk):
            to_core(t).wait_send()

        def db_out(t, m, slot, b):
            return pltpu.make_async_copy(
                stage.at[slot, :, at(b, width)], d_ref.at[1, at(m, mt), at(b * n_chunk + t, width)], dbs.at[slot, b])

        def grads(t):
            def rows_of(m):
                slot = odd(m)

                @pl.when(t * m_steps + m >= 2)
                def _():
                    for b in BOTH:
                        db_out(t, m, slot, b).wait()

                db = mm(zh[0, at(m, mt)], g[t]) * scale
                stage[slot] = db
                own = both(1, at(m, mt), t)
                sums = two_sums(db, db * own.astype(F32))
                for b in BOTH:
                    acc[1, :2, at(b * n_chunk + t, width)] += sums[:, b * width:(b + 1) * width]
                    db_out(t, m, slot, b).start()
                da[at(m, mt)] = jnp.where(t == 0, 0.0, da[at(m, mt)]) + mm_bt(own, g[t])

            loop(m_steps, rows_of)

        def at_first(t):
            to_first(t).wait_recv()
            ck[:, group(t, bit1)] += r1[t]
            to_second(t).start()
            pl.when(t + 2 < n_chunk)(lambda: to_first(t + 2).start())

        def at_second(t):
            to_second(t).wait_recv()
            corr_mat = (ck[at(bit2, quart), group(t, bit1)] + r2[t]) * scale
            row_ids = (2 * c + bit2) * quart + lax.broadcasted_iota(jnp.int32, (quart, width), 0)
            col_ids = (bit1 * n_chunk + t) * width + lax.broadcasted_iota(jnp.int32, (quart, width), 1)
            is_diag = row_ids == col_ids
            lam_val = lam_ref[0]
            loss = jnp.where(is_diag, (1.0 - corr_mat) * (1.0 - corr_mat), lam_val * corr_mat * corr_mat)
            acc[0, 2:3, :width] += jnp.sum(loss, axis=0, keepdims=True)
            grad = jnp.where(is_diag, -2.0 * (1.0 - corr_mat), 2.0 * lam_val * corr_mat).astype(BF16)
            g[t, at(2 * c + bit2, quart), at(bit1, width)] = grad
            g_second(t, bit2).start()

        def back_second(t):
            g_second(t, other(bit2)).wait_recv()
            g_first(t, bit1).start()

        def back_first(t):
            g_first(t, other(bit1)).wait_recv()
            g_core(t, c).start()

        def back_core(t):
            g_core(t, other(c)).wait_recv()
            grads(t)

        stages = (at_first, at_second, back_second, back_first, back_core)

        def advance(tau):
            for lag, stage_fn in enumerate(stages):
                t = tau - lag
                pl.when(jnp.logical_and(t >= 0, t < n_chunk))(lambda t=t, stage_fn=stage_fn: stage_fn(t))

        loop(n_chunk + len(stages) - 1, advance)

        def da_out(m):
            return pltpu.make_async_copy(da.at[at(m, mt)], d_ref.at[0, at(m, mt)], das.at[m])

        def finish(m):
            d = da[at(m, mt)] * scale
            da[at(m, mt)] = d
            acc[0, :2] += two_sums(d, d * zh[0, at(m, mt)].astype(F32))
            da_out(m).start()

        share.start(1)
        loop(m_steps, finish)
        share.start(0)
        for t in range(n_chunk):
            for copy in (to_first(t), to_second(t), g_second(t, bit2), g_first(t, bit1), g_core(t, c)):
                copy.wait_send()
        for b in BOTH:
            so_ref[b] = share.total(b)
            for slot in BOTH:
                db_out(0, 0, slot, b).wait()
        for i in range(z_steps):
            zh_out(i // (z_steps // 2), i % (z_steps // 2), i).wait()
        for m in range(m_steps):
            da_out(m).wait()

    return call(
        kernel, "corr_grad", 3, (), [ANY, VMEM, pl.BlockSpec(memory_space=pltpu.SMEM)], [ANY, ANY, VMEM],
        [sds((2, rows, dim), BF16), sds((2, rows, dim), F32), sds((2, 4, dim), F32)],
        [pltpu.VMEM((2, rows, dim), BF16), pltpu.VMEM((rows, dim), F32), pltpu.VMEM((half, dim), F32),
         pltpu.VMEM((n_chunk, half, width), F32), pltpu.VMEM((n_chunk, quart, width), F32),
         pltpu.VMEM((n_chunk, dim, pair), BF16), pltpu.VMEM((2, mt, pair), F32)] + Share.scratch(2, 4, dim)
        + [TWO_DMA, DMA((z_steps,))] + [DMA((n_chunk,))] * 12 + [DMA((2, 2)), DMA((m_steps,))],
        all_rows * dim * dim * 3, all_rows * dim * 12, (z, sums, lam))


def backward(d_emb, zh, sz, s_emb, layers, x2, h_a, h_b, total):
    all_rows, dim = zh.shape
    rows, half = all_rows // 2, dim // 2
    width = 256
    slabs = dim // width
    items = 2 * slabs
    piece = half // 2
    n_layer = len(layers) + 1
    n_chunk = n_layer * slabs
    (u2, s2, gb2, w3_t, x1), (u1, s1, gb1, w2_t, _) = layers

    def kernel(d_ref, zh_ref, sz_ref, sd_ref, x2_ref, x1_ref, ha_ref, hb_ref, u2_ref, u1_ref, w3_ref, w2_ref,
               s2_ref, s1_ref, gb2_ref, gb1_ref, dw3_ref, dw2_ref, dw1_ref, sum_ref, du_ref, part_ref, ry_ref, rx_ref,
               dbuf, xbuf, wbuf, ubuf, dybuf, dubuf, psend, pkeep, dr, ebuf, mbuf, fbuf, acc, got, ssem, rsem,
               us, ws, xl, dl, dus, ps, pr, pm, ys, yr, xs, xr, es, fs, fcs, fcr, credit):
        share = Share(acc, got, ssem, rsem)
        here = coords()
        y, x, c = here
        ypeer, xpeer, cpeer = flip(here, Y_PEER), flip(here, X_PEER), flip(here, C_PEER)
        arrive()

        def column(k, n):
            side = odd(n + jnp.where(k == 0, other(y), 0))
            return jnp.where(k == 1, n, side * (slabs // 2) + lax.div(n, 2))

        def turn(k):
            return jnp.where(k == 0, 0, other(y))

        def m_slot(j):
            return lax.rem(j, 4)

        def copy(src, dst, sem):
            return pltpu.make_async_copy(src, dst, sem)

        def to_core(s):
            return remote(psend.at[odd(s)], dr.at[odd(s)], ps.at[s], pr.at[s], cpeer)

        def keep_out(s):
            return copy(pkeep.at[odd(s)], part_ref.at[s], pm)

        def chip_sum(s):
            slot = odd(s)
            to_core(s).wait_recv()
            pkeep[slot] += dr[slot]

            @pl.when(s + 2 < n_chunk)
            def _():
                pl.semaphore_signal(credit, inc=1, device_id=device(cpeer), device_id_type=pl.DeviceIdType.MESH)

            to_core(s).wait_send()
            keep_out(s).start()

        def to_y(src, j):
            return remote(src, ry_ref.at[j], ys.at[lax.div(j, slabs)], yr.at[j], ypeer)

        def issue(s):
            keep_out(s).wait()
            k = lax.div(s, slabs)

            @pl.when(k == 1)
            def _():
                to_y(part_ref.at[s, at(other(y), piece)], s).start()

            @pl.when(jnp.logical_and(k != 1, odd(s) == turn(k)))
            def _():
                for b in BOTH:
                    to_y(part_ref.at[s, at(b, piece)], s - turn(k) + b).start()

        def to_x(j):
            return remote(mbuf.at[m_slot(j)], rx_ref.at[j], xs.at[m_slot(j)], xr.at[j], xpeer)

        def result(j, k):
            j = lax.rem(j, slabs)
            if k == 1:
                return dw2_ref.at[at(c, piece), at(j, width)]
            return (dw1_ref if k else dw3_ref).at[at(2 * c + odd(j), piece), at(lax.div(j, 2), width)]

        def put(j, k):
            slot = odd(j)
            return (copy(fbuf.at[slot], result(j, k), fs.at[slot]),
                    remote(fbuf.at[slot], result(j, k), fcs.at[slot], fcr.at[k], cpeer))

        def put_done(j):
            here_copy, there_copy = put(j, 0)
            here_copy.wait()
            there_copy.wait_send()

        def load_y(j):
            return copy(ry_ref.at[j], ebuf.at[0], es.at[0])

        def load_own(j):
            k = lax.div(j, slabs)
            s = jnp.where(k == 1, j, 2 * lax.div(j, 2) + 1 - turn(k))
            row = jnp.where(k == 1, y, odd(j))
            return copy(part_ref.at[s, at(row, piece)], ebuf.at[1], es.at[1])

        def load_x(j):
            return copy(rx_ref.at[j], ebuf.at[2], es.at[2])

        def fetch_x(j):
            to_x(j).wait_recv()
            load_x(j).start()

        def begin(j):
            to_y(ry_ref.at[j], j).wait_recv()
            load_y(j).start()
            load_own(j).start()
            pl.when(j >= 2)(lambda: fetch_x(j - 2))

        def deliver(j):
            load_x(j).wait()

            pl.when(j >= 2)(lambda: put_done(j))
            slot = odd(j)
            fbuf[slot] = mbuf[m_slot(j)] + ebuf[2]
            for k in range(n_layer):
                @pl.when(lax.div(j, slabs) == k)
                def _(k=k):
                    for one in put(j, k):
                        one.start()

        def end(j):
            load_y(j).wait()
            load_own(j).wait()
            pl.when(j >= 4)(lambda: to_x(j).wait_send())
            mbuf[m_slot(j)] = ebuf[0] + ebuf[1]
            to_x(j).start()
            pl.when(j >= 2)(lambda: deliver(j - 2))

        def begun(q):
            early = jnp.maximum(lax.div(q - 1, 4) - 1, 0)
            late = 2 + lax.div(4 * (q - items) + 5, 9)
            return jnp.where(q < items, early, late)

        def events(q):
            now, before, earlier = begun(q), begun(q - 1), begun(q - 2)
            pl.when(before > earlier)(lambda: end(before - 1))
            pl.when(now > before)(lambda: begin(now - 1))

        def left(v, natural, part):
            first = jnp.where(natural, part, 2 * part)
            second = jnp.where(natural, 2 + part, 2 * part + 1)
            return jnp.concatenate([xbuf[at(v, rows), at(b, piece)] for b in (first, second)], axis=1)

        def weight_slab(s, v, natural, d):
            slot = odd(s)
            pl.when(jnp.logical_and(v == 0, s > 0))(lambda: chip_sum(s - 1))
            pl.when(jnp.logical_and(v == 1, s > 0))(lambda: issue(s - 1))
            for buf, part in ((psend, other(c)), (pkeep, c)):
                buf[slot] = jnp.where(v == 0, 0.0, buf[slot]) + mm_at(left(v, natural, part), d)

            @pl.when(v == 1)
            def _():
                pl.when(s >= 2)(lambda: pl.semaphore_wait(credit, 1))
                to_core(s).start()

        def emb_loads(i):
            n, v = split(i)
            cols = at(column(0, n), width)
            return (copy(d_ref.at[at(v, rows), cols], ubuf.at[v], us.at[v]),
                    copy(zh_ref.at[at(v, rows), cols], wbuf.at[v], ws.at[v]))

        def x_load(src, v, src_at):
            return copy(src.at[at(src_at, rows)], xbuf.at[at(v, rows)], xl.at[v])

        def u_load(layer, i, ref=u2_ref):
            slot = lax.rem(layer * items + i, 3)
            n, v = split(i)
            cols = at(column(layer + 1, n), width)
            return copy(ref.at[at(v, rows), cols], ubuf.at[slot], us.at[slot])

        def w_load(layer, n, ref=w3_ref):
            slot = odd(n)
            return copy(ref.at[:, at(column(layer + 1, n), width)], wbuf.at[slot], ws.at[slot])

        def start_u(layer, i):
            for k, ref in enumerate((u2_ref, u1_ref)):
                pl.when(layer == k)(lambda ref=ref: u_load(layer, i, ref).start())

        def start_w(layer, n):
            for k, ref in enumerate((w3_ref, w2_ref)):
                pl.when(layer == k)(lambda ref=ref: w_load(layer, n, ref).start())

        x_load(x2_ref, 0, 0).start()
        for one in emb_loads(0):
            one.start()
        x_load(x2_ref, 1, 1).start()
        all_arrived()

        def emb_item(i):
            n, v = split(i)

            @pl.when(i + 1 < items)
            def _():
                for one in emb_loads(i + 1):
                    one.start()

            @pl.when(i + 1 == items)
            def _():
                u_load(0, 0).start()
                w_load(0, 0).start()

            pl.when(i < 2)(lambda: x_load(x2_ref, v, v).wait())
            for one in emb_loads(i):
                one.wait()
            events(i)
            cols = at(column(0, n), width)
            _, inv = mean_inv(sz_ref[v, :, cols], total)
            sd = sd_ref[v, :2, cols] / total
            d = (inv * (ubuf[v] - sd[:1] - wbuf[v].astype(F32) * sd[1:])).astype(BF16)
            dbuf[at(v, rows), cols] = d
            weight_slab(n, v, False, d)

        loop(items, emb_item)
        for v in BOTH:
            x_load(x1_ref, v, v).start()

        def du_out(i):
            n, v = split(i)
            return copy(dubuf.at[v], du_ref.at[at(v, rows), at(n, width)], dus.at[v])

        most = pl.ds(0, dim - width)
        d_reload = lambda: copy(du_ref.at[:, most], dbuf.at[:, most], dl)

        def stats(layer, v, cols):
            pick = lambda one, two: jnp.where(layer == 0, one, two)
            mean, inv = mean_inv(pick(s2_ref[v, :, cols], s1_ref[v, :, cols]), total)
            gb = pick(gb2_ref[:, cols], gb1_ref[:, cols])
            return mean, inv, gb[:1], gb[1:]

        def step(layer, s):
            natural = layer == 0

            @pl.when(s < items)
            def _():
                i = s
                n, v = split(i)
                g = layer * items + i
                cols = at(column(layer + 1, n), width)
                pl.when(i + 1 < items)(lambda: start_u(layer, i + 1))
                pl.when(jnp.logical_and(v == 0, n + 1 < slabs))(lambda: start_w(layer, n + 1))

                @pl.when(jnp.logical_and(i + 1 == items, natural))
                def _():
                    u_load(1, 0, u1_ref).start()
                    w_load(1, 0, w2_ref).start()

                pl.when(jnp.logical_and(i == 0, layer == 1))(lambda: d_reload().wait())
                u_load(layer, i).wait()
                pl.when(v == 0)(lambda: w_load(layer, n).wait())
                dx = mm(dbuf[at(v, rows)], wbuf[odd(n)])
                mean, inv, gamma, beta = stats(layer, v, cols)
                norm = (ubuf[lax.rem(g, 3)] - mean) * inv
                dy = jnp.where(norm * gamma + beta > 0, dx, 0.0)
                dybuf[v] = dy
                acc[g] = two_sums(dy, dy * norm)
                share.start(g)

                @pl.when(jnp.logical_and(i + 1 == items, natural))
                def _():
                    for one in BOTH:
                        du_out(one).wait()
                    d_reload().start()

            @pl.when(s > 0)
            def _():
                i = s - 1
                n, v = split(i)
                g = layer * items + i
                cols = at(column(layer + 1, n), width)
                pl.when(jnp.logical_and(n == 0, natural))(lambda: x_load(x1_ref, v, v).wait())
                pl.when(jnp.logical_and(n == 0, layer == 1))(lambda: x_load(ha_ref, v, y).wait())
                events(items + g)
                tot = share.total(g)
                sum_ref[layer, v, :, cols] = tot
                mean, inv, gamma, _ = stats(layer, v, cols)
                tot = tot / total
                slope = inv * tot[1:]
                d = (gamma * inv * (dybuf[v] - (tot[:1] + (ubuf[lax.rem(g, 3)] - mean) * slope))).astype(BF16)

                @pl.when(jnp.logical_and(natural, n + 1 < slabs))
                def _():
                    pl.when(n > 0)(lambda: du_out(i).wait())
                    dubuf[v] = d
                    du_out(i).start()

                @pl.when(jnp.logical_and(natural, n + 1 == slabs))
                def _():
                    dbuf[at(v, rows), cols] = d

                weight_slab((layer + 1) * slabs + n, v, natural, d)

            @pl.when(jnp.logical_and(s == items, natural))
            def _():
                x_load(ha_ref, 0, y).start()
                x_load(hb_ref, 1, y).start()

        def layer_steps(k):
            layer = lax.div(k, items + 1)
            step(layer, k - layer * (items + 1))

        loop(len(layers) * (items + 1), layer_steps)

        last = n_chunk - 1
        chip_sum(last)
        issue(last)
        done = 16
        end(done - 1)

        def tail(j):
            begin(j)
            end(j)

        loop(n_chunk, tail, done)
        for j in (last - 1, last):
            fetch_x(j)
            deliver(j)
        put_done(0)
        put_done(1)
        for k in range(n_layer):
            theirs = dw2_ref.at[at(other(c), piece)] if k == 1 else (dw1_ref if k else dw3_ref).at[at(other(c), half)]
            remote(theirs, theirs, fcs.at[0], fcr.at[k], cpeer).wait_recv()
            sent = ry_ref.at[at(k, slabs)]
            remote(sent, sent, ys.at[k], yr.at[0], ypeer).wait_send()
        for j in range(n_chunk - 4, n_chunk):
            to_x(j).wait_send()

    n_item = len(layers) * items
    vm = lambda *shape: pltpu.VMEM(shape, F32)
    bf = lambda *shape: pltpu.VMEM(shape, BF16)
    return call(
        kernel, "backward", 4, (),
        [ANY, ANY, VMEM, VMEM] + [ANY] * 8 + [VMEM] * 4, [ANY] * 3 + [VMEM] + [ANY] * 4,
        [sds((dim, half), F32), sds((half, dim), F32), sds((dim, half), F32), sds((len(layers), 2, 2, dim), F32),
         sds((all_rows, dim), BF16), sds((n_chunk, half, width), F32), sds((n_chunk, piece, width), F32),
         sds((n_chunk, piece, width), F32)],
        [bf(all_rows, dim), bf(all_rows, dim), bf(2, dim, width), vm(3, rows, width), vm(2, rows, width), bf(2, rows, width),
         vm(2, half, width), vm(2, half, width), vm(2, half, width), vm(3, piece, width), vm(4, piece, width),
         vm(2, piece, width)] + Share.scratch(n_item, 2, width)
        + [DMA((3,)), TWO_DMA, TWO_DMA, DMA, TWO_DMA, DMA((n_chunk,)), DMA((n_chunk,)), DMA, DMA((n_layer,)),
           DMA((n_chunk,)), DMA((4,)), DMA((n_chunk,)), DMA((3,)), TWO_DMA, TWO_DMA, DMA((n_layer,)),
           pltpu.SemaphoreType.REGULAR],
        all_rows * dim * dim * 10, all_rows * dim * 40,
        (d_emb, zh, sz, s_emb, x2, x1, h_a, h_b, u2, u1, w3_t, w2_t, s2, s1, gb2, gb1))


def settle(*grads):
    steps = 8

    def kernel(*refs):
        for src, dst in zip(refs[:len(grads)], refs[len(grads):]):
            dst[...] = src[...]

    specs = [pl.BlockSpec((g.shape[0] // steps, g.shape[1]), lambda i: (i, 0)) for g in grads]
    return call(kernel, "settle", None, (steps,), specs, specs, [sds(g.shape, F32) for g in grads], [], 0,
                len(grads) * grads[0].size * 8, grads)


def solution(mesh):
    def shard_body(h_a, h_b, w_one, w_two, w_three, g_one, b_one, g_two, b_two, lam_off):
        y = lax.axis_index('model')
        total = float(h_a.shape[0] * mesh.shape['data'])
        dim, half = w_three.shape
        gb2 = jnp.stack([g_two, b_two])
        u1, s1, gb1, w_two_o = fwd_first(h_a, h_b, w_one, w_two, jnp.stack([g_one, b_one]))
        x1, u2, s2, w2_t, w_three_o = fwd_next(u1, s1, gb1, w_two, w_two_o, True, total, 1, w_three)
        x2, z, sz, w3_t = fwd_next(u2, s2, gb2, w_three, w_three_o, False, total, 2)
        zh, d_emb, s_emb = corr_grad(z, sz, lam_off, total)
        loss = jnp.sum(s_emb[0, 2])
        dw_three, dw_two, dw_one, sums, *_ = backward(
            d_emb.reshape(z.shape), zh.reshape(z.shape), sz, s_emb,
            ((u2, s2, gb2, w3_t, x1), (u1, s1, gb1, w2_t, None)), x2, h_a, h_b, total)
        dw_three, dw_two, dw_one = settle(dw_three, dw_two, dw_one)
        sums = jnp.sum(sums, axis=1)
        sum2 = sums[0]
        sum1 = lax.dynamic_slice_in_dim(sums[1], y * half, half, 1)
        return loss.reshape(1), dw_one, dw_two, dw_three, sum1[1], sum1[0], sum2[1], sum2[0]

    in_specs = (P('data', None), P('data', None), P(None, 'model'), P('model', None), P(None, 'model'),
                P('model'), P('model'), P(), P(), P())
    out_specs = (P(), P(None, 'model'), P('model', None), P(None, 'model'), P('model'), P('model'), P(), P())
    return jax.shard_map(shard_body, mesh=mesh, in_specs=in_specs, out_specs=out_specs, check_vma=False)
```

time: 4710 us -> 883 us (0.19)
  waiting for transfers between devices: 3950 us -> 0 us
  Pallas kernels: 0 us -> 874 us
  matrix products: 447 us -> 0 us
  other arithmetic: 193 us -> 4.92 us
  blocking collectives: 73.6 us -> 0 us
    psum x4 -> x0, waiting for transfers between devices: 3410 us -> none  [the longest x1 1450 us: shard_body(): lax.psum(jnp.einsum('woe,ef->wof', act_one, w_two, preferred_element_type...]
    pallas_call x0 -> x6, Pallas kernels: none -> 874 us  [call(): pl.pallas_call(kernel, name=name, grid=grid, in_specs=in_specs, out_specs...]
    dot_general x11 -> x0, matrix products: 447 us -> none  [the longest x1 51.4 us: shard_body(): jnp.einsum('wof,ef->woe', d_pre_two, w_two, preferred_element_type=jnp.fl...]
    reduce_scatter x1 -> x0, waiting for transfers between devices: 340 us -> none  [shard_body(): lax.psum_scatter(d_part_b, 'model', scatter_dimension=1, tiled=True)]
    all_gather x1 -> x0, waiting for transfers between devices: 198 us -> none  [shard_body(): emb_b_full = lax.all_gather(embed_bf[1], 'model', axis=1, tiled=True)]
    convert_element_type x3 -> x0, other arithmetic: 100 us -> none  [the longest x1 53.6 us: bn_backward(): d_pre.astype(jnp.bfloat16)]
    reduce_sum x6 -> x2, other arithmetic: 91.2 us -> 2.26 us  [the longest x1 1.38 us: shard_body(): loss = jnp.sum(s_emb[0, 2])]
    psum x7 -> x0, blocking collectives: 73.6 us -> none  [the longest x3 35.1 us: batch_norm(): moments = lax.psum(local_sums, 'data') / total_rows]
  transfers between devices with their start and end apart: 6 -> 0, of which waited for: 6 -> 0; matrix products, arithmetic and copies ran while one was open for 2% -> 0% of each run, Pallas kernels for 0% -> 0%
where the time goes in v1:
time: 883 us; the launch traced here: 881 us
  Pallas kernels  874 us (99%)
    pallas_call x6, Pallas kernels, call(): pl.pallas_call(kernel, name=name, grid=grid, in_specs=in_specs, out_specs...  874 us

profile of v1, /device:TPU:0, one launch (start us, length us, event | category | flops | bytes accessed | tf_op | source)
XLA Modules:
  0.0 881.5 jit_solution(18241791454393400610)
XLA Ops:
  0.6 1.3 pad_maximum_fusion.1.gb_ref
  1.9 74.2 %fwd_first.1 = (f32[4096,2048]{1,0:T(8,128)}, f32[2,2,2048]{2,1,0:T(2,128)}, f32[2,2048]{1,0:T(2,128)}, bf16[1024,2048]{1,0:T(8,128)(2,1)}) custom-call(bf16[4096,2048]{1,0:T(8,128)(2,1)} %ha_ref.3, bf16[4096,2048]{1,0:T(8,128)(2,1)} %hb_ref.3, bf16[2048,1024]{1,0:T(8,128)(2,1)} %w_ref.1, bf16[1024,2048]{1,0:T(8,128)(2,1)} %wo_ref.2, ...), custom_call_target="tpu_custom_call" | custom-call | flops 34359738368 | bytes 100663296 | tf_op jit(solution)/shard_map/fwd_first/pallas_call | solution.py:194
  76.2 53.7 %fwd_next.2 = (bf16[4096,2048]{1,0:T(8,128)(2,1)}, f32[4096,2048]{1,0:T(8,128)}, f32[2,2,2048]{2,1,0:T(2,128)}, bf16[2048,2048]{1,0:T(8,128)(2,1)}, bf16[2048,1024]{1,0:T(8,128)(2,1)}) custom-call(f32[4096,2048]{1,0:T(8,128)} %get-tuple-element.31.u_ref.u1_ref, f32[2,2,2048]{2,1,0:T(2,128)} %get-tuple-element.32.s_ref.s1_ref, ...), custom_call_target="tpu_custom_call" | custom-call | flops 34359738368 | bytes 83886080 | tf_op jit(solution)/shard_map/fwd_next/pallas_call | solution.py:194
  129.8 1.3 pad_maximum_fusion.gb_ref.gb2_ref
  131.2 49.9 %fwd_next.3 = (bf16[4096,2048]{1,0:T(8,128)(2,1)}, f32[4096,2048]{1,0:T(8,128)}, f32[2,2,2048]{2,1,0:T(2,128)}, bf16[2048,2048]{1,0:T(8,128)(2,1)}) custom-call(f32[4096,2048]{1,0:T(8,128)} %get-tuple-element.35.u_ref.u2_ref, f32[2,2,2048]{2,1,0:T(2,128)} %get-tuple-element.36.s_ref.s2_ref, f32[2,2048]{1,0:T(2,128)} %pad_maximum_fusion.gb_ref.gb2_ref, ...), custom_call_target="tpu_custom_call" | custom-call | flops 34359738368 | bytes 83886080 | tf_op jit(solution)/shard_map/fwd_next/pallas_call | solution.py:194
  181.7 160.6 %corr_grad.1 = (bf16[2,2048,2048]{2,1,0:T(8,128)(2,1)}, f32[2,2048,2048]{2,1,0:T(8,128)}, f32[2,4,2048]{2,1,0:T(4,128)}) custom-call(f32[4096,2048]{1,0:T(8,128)} %get-tuple-element.38.z_ref, f32[2,2,2048]{2,1,0:T(2,128)} %get-tuple-element.39.s_ref.sz_ref, f32[1]{0:T(128)S(6)} %copy.18.lam_ref), custom_call_target="tpu_custom_call" | custom-call | flops 51539607552 | bytes 100663296 | tf_op jit(solution)/shard_map/corr_grad/pallas_call | solution.py:194
  342.3 517.5 %backward.1 = (f32[2048,1024]{1,0:T(8,128)}, f32[1024,2048]{1,0:T(8,128)}, f32[2048,1024]{1,0:T(8,128)}, f32[2,2,2,2048]{3,2,1,0:T(2,128)}, bf16[4096,2048]{1,0:...) custom-call(f32[4096,2048]{1,0:T(8,128)} %bitcast.19, ...), custom_call_target="tpu_custom_call" | custom-call | flops 171798691840 | bytes 335544320 | tf_op jit(solution)/shard_map/backward/pallas_call | solution.py:194
  859.8 18.1 %settle.1 = (f32[2048,1024]{1,0:T(8,128)}, f32[1024,2048]{1,0:T(8,128)}, f32[2048,1024]{1,0:T(8,128)}) custom-call(f32[2048,1024]{1,0:T(8,128)} %get-tuple-element.47.refs_0_, f32[1024,2048]{1,0:T(8,128)} %get-tuple-element.48.refs_1_, f32[2048,1024]{1,0:T(8,128)} %get-tuple-element.49.refs_2_), custom_call_target="tpu_custom_call" | custom-call | bytes 50331648 | tf_op jit(solution)/shard_map/settle/pallas_call | solution.py:194
  877.9 0.9 reduce_sum.19
  878.8 0.7 constant_dynamic-slice_fusion.1
  879.5 0.6 fusion
  880.1 1.4 slice_reduce_fusion
  (1 shorter events, 0.0 us)
